TPU v7x, 32 devices: a whole 2x2x4 slice. The times are simulated.
32 devices in a mesh: dp: 4 (over x, y), sp: 8 (over z, core).
Axes of the slice: x: 2, y: 2, z: 4, core: 2. Of those that a mesh axis runs over, the one named last changes fastest.
Arguments:
- q: bfloat16 [128, 24, 128], P('dp'), parts along dimension 0
- k: bfloat16 [128, 8192, 8, 128], P('dp', 'sp'), parts along dimension 0
- v: bfloat16 [128, 8192, 8, 128], P('dp', 'sp'), parts along dimension 0
Outputs:
- q: bfloat16 [128, 24, 128], P('dp'), parts along dimension 0
There are 4 independent parts. A program takes and returns all parts, laid end to end along the dimension named above; each array names one.
All inputs are finite; a program needn't handle non-finite values.
Results may differ from a plain program's by a relative error of at most 0.012.
Values are sent between devices in bfloat16 or wider.
A program may use at most 2 GiB of HBM per device.

v0:
```python
import jax
import jax.numpy as jnp
from jax import lax
from jax.sharding import PartitionSpec as P


def einsum(form, a, b):
    return jnp.einsum(form, a.astype(jnp.float32), b.astype(jnp.float32))


def part_of(q, k, v):
    grouped = q.reshape(q.shape[0], k.shape[2], -1, q.shape[2])
    scores = einsum("bgsd,bugd->bgsu", grouped, k) * q.shape[2] ** -0.5
    high = jnp.max(scores, -1, keepdims=True)
    weights = jnp.exp(scores - high)
    seen = einsum("bgsu,bugd->bgsd", weights.astype(jnp.bfloat16), v)
    return jnp.concatenate([seen, jnp.sum(weights, -1, keepdims=True), high], -1)


def together(parts):
    seen, total, high = parts[..., :-2], parts[..., -2:-1], parts[..., -1:]
    scale = jnp.exp(high - jnp.max(high, 0))
    return (jnp.sum(seen * scale, 0) / jnp.sum(total * scale, 0)).astype(jnp.bfloat16)


def solution(mesh):
    def step(q, k, v):
        return together(lax.all_gather(part_of(q, k, v), "sp")).reshape(q.shape)

    return jax.shard_map(
        step,
        mesh=mesh,
        in_specs=(P("dp", None, None), P("dp", "sp", None, None), P("dp", "sp", None, None)),
        out_specs=P("dp", None, None),
        check_vma=False,
    )
```

profile of v0, /device:TPU:0, one launch (start us, length us, event | category | flops | bytes accessed | tf_op | source)
XLA Modules:
  0.0 156.7 jit_solution(11094111857638591864)
XLA Ops:
  6.5 0.0 all-gather.3.cloned.1.call-start
  6.5 1.0 copy.46
  7.5 26.1 %multiply_reduce_fusion = (f32[32,8,3]{2,1,0:T(8,128)S(1)}, f32[32,8,3,1024]{3,2,1,0:T(4,128)S(1)}) fusion(bf16[32,1024,8,128]{3,2,1,0:T(8,128)(2,1)} %param.4, bf16[32,8,3,128]{3,0,2,1:T(8,128)(2,1)S(1)} %bitcast.15), kind=kOutput, calls=%fused_computation.5 | convolution fusion | flops 202898688 | bytes 70454272 | tf_op jit(solution)/shard_map/bgsd,bugd->bgsu/dot_general | solution.py:8
  33.6 0.0 copy-start
  33.6 1.9 %copy-done = f32[32,8,3,1024]{3,2,1,0:T(4,128)} copy-done((f32[32,8,3,1024]{3,2,1,0:T(4,128)}, f32[32,8,3,1024]{3,2,1,0:T(4,128)S(1)}, u32[]{:S(2)}) %copy-start) | copy-done | bytes 3145752
  35.6 2.1 %fusion.5 = f32[32,8,3]{2,1,0:T(8,128)S(1)} fusion(f32[32,8,3,1024]{3,2,1,0:T(4,128)S(1)} %get-tuple-element.11, f32[32,8,3]{2,1,0:T(8,128)S(1)} %get-tuple-element.10), kind=kLoop, calls=%fused_computation.8 | loop fusion | flops 2358528 | bytes 3151872 | tf_op jit(solution)/shard_map/reduce_sum | solution.py:17
  37.7 26.7 %fusion = f32[32,8,3,128]{3,2,1,0:T(4,128)S(1)} fusion(bf16[32,1024,8,128]{3,2,1,0:T(8,128)(2,1)} %param.5, f32[32,8,3,1024]{3,2,1,0:T(4,128)} %copy-done, f32[32,8,3]{2,1,0:T(8,128)S(1)} %get-tuple-element.10), kind=kOutput, calls=%fused_computation | convolution fusion | flops 203685888 | bytes 70650880 | tf_op jit(solution)/shard_map/bgsu,bugd->bgsd/dot_general | solution.py:8
  64.4 1.7 %copy.52 = f32[32,8,3,1]{3,2,1,0:T(4,128)S(1)} copy(f32[32,8,3,1]{2,1,0,3:T(8,128)S(1)} %bitcast.16) | data formatting | bytes 6144 | tf_op jit(solution)/shard_map/broadcast_in_dim | solution.py:17
  66.0 1.7 %copy.53 = f32[32,8,3,1]{3,2,1,0:T(4,128)S(1)} copy(f32[32,8,3,1]{2,1,0,3:T(8,128)S(1)} %bitcast.14) | data formatting | bytes 6144 | tf_op jit(solution)/shard_map/broadcast_in_dim | solution.py:14
  67.7 0.4 pad_maximum_fusion
  68.1 1.0 copy.54
  69.2 0.0 all-gather.3.cloned.1.call-update
  69.2 66.9 %all-gather.3.cloned.1.call-done = f32[256,8,3,130]{3,1,2,0:T(8,128)} async-done(((f32[32,8,3,130]{3,1,2,0:T(8,128)}), f32[256,8,3,130]{3,1,2,0:T(8,128)}) %all-gather.3.cloned.1.call-update) | async-done | bytes 3194896 | tf_op jit(solution)/shard_map/all_gather | solution.py:28
  136.1 5.7 %fusion.14 = (f32[8,32,8,3,1]{4,2,3,1,0:T(8,128)}, f32[32,8,3]{1,2,0:T(4,128)S(1)}, f32[8,32,8,3,1]{4,2,3,1,0:T(8,128)S(1)}) fusion(f32[8,32,8,3,130]{4,2,3,1,0:T(8,128)} %bitcast.12), kind=kLoop, calls=%fused_computation.21 | loop fusion | flops 5376 | bytes 101376 | tf_op jit(solution)/shard_map/slice | solution.py:21
  141.9 2.7 %copy.68 = f32[8,32,8,3,1]{1,2,4,3,0:T(8,128)S(1)} copy(f32[8,32,8,3,1]{4,2,3,1,0:T(8,128)} %get-tuple-element.5) | data formatting | bytes 49152
  144.5 0.1 copy.70
  144.6 1.5 copy.67
  146.2 0.2 copy.56
  146.4 2.4 %fusion.4 = f32[32,8,3,128]{3,1,2,0:T(8,128)S(1)} fusion(f32[8,32,8,3,130]{4,2,3,1,0:T(8,128)} %bitcast.13, f32[8,32,8,3]{2,3,1,0:T(4,128)S(1)} %copy.56), kind=kLoop, calls=%fused_computation.7 | loop fusion | flops 1474560 | bytes 3563520 | tf_op jit(solution)/shard_map/reduce_sum | solution.py:23
  148.9 0.1 copy.58
  149.0 0.2 fusion.10
  149.1 0.8 copy.61
  (3 shorter events, 0.1 us)
Async XLA Ops:
  6.5 129.6 %all-gather.3.cloned.1.call-start = ((), (), s32[]{:S(2)}) async-start(), calls=%async_computation | async-start | bytes 7077888 | tf_op jit(solution)/shard_map/all_gather | solution.py:28
  33.6 1.9 %copy-start = (f32[32,8,3,1024]{3,2,1,0:T(4,128)}, f32[32,8,3,1024]{3,2,1,0:T(4,128)S(1)}, u32[]{:S(2)}) copy-start(f32[32,8,3,1024]{3,2,1,0:T(4,128)S(1)} %get-tuple-element.11) | copy-start | bytes 9437188
Sparse Core Ops, SparseCore 0:
  69.3 66.7 all-gather.2
where the time goes:
time: 157 us
  waiting for transfers between devices  67 us (43%)
  matrix products  52.8 us (34%)
  between operations  13.5 us (9%)
  local copies, waits for them, and re-layouts  12.6 us (8%)
  other arithmetic  10.9 us (7%)
    all_gather x1, waiting for transfers between devices, step(): return together(lax.all_gather(part_of(q, k, v), 'sp')).reshape(q.shape)  66.9 us
    dot_general x2, matrix products, einsum(): return jnp.einsum(form, a.astype(jnp.float32), b.astype(jnp.float32))  52.8 us
    unnamed x6, local copies, waits for them, and re-layouts  7.13 us
    slice x1, other arithmetic, together(): seen, total, high = (parts[..., :-2], parts[..., -2:-1], parts[..., -1:])  5.73 us
  transfers between devices with their start and end apart: 1, of which 1 were waited for; matrix products, arithmetic and copies ran while one was open for 0% of the time, Pallas kernels for 0%

commit v1 on v0

v1 whole, which is shorter than its diff:
```python
import functools
import math

import jax
import jax.numpy as jnp
from jax import lax
from jax.experimental import pallas as pl
from jax.experimental.pallas import tpu as pltpu
from jax.sharding import PartitionSpec as P

MESH = pl.DeviceIdType.MESH
LANES = 128
SLOTS = 6
LAG = 6
TAIL = 8


def kernel(n, kv_heads, q_ref, k_ref, v_ref, o_ref, k_buf, v_buf, s_buf, w_buf, m_buf, parts, stats, k_sem, v_sem, ps_sem, pr_sem, ss_sem, sr_sem, os_sem, or_sem):
    split = q_ref.shape[0] - TAIL
    batch, heads, head = q_ref.shape
    rows = k_ref.shape[1]
    half = rows // 2
    quarter = rows // 4
    blocks = half // LANES
    c = head**-0.5 * math.log2(math.e)
    me = lax.axis_index("sp")

    def k_copy(i):
        return pltpu.make_async_copy(k_ref.at[i], k_buf.at[lax.rem(i, SLOTS)], k_sem.at[lax.rem(i, SLOTS)])

    def v_copy(i, part):
        at = pl.ds(part * half, half)
        slot = lax.rem(i, SLOTS)
        return pltpu.make_async_copy(v_ref.at[i, at], v_buf.at[slot, at], v_sem.at[slot, part])

    row = lax.broadcasted_iota(jnp.int32, (heads, LANES), 0)
    lane = lax.broadcasted_iota(jnp.int32, (heads, LANES), 1)
    own = lax.rem(lane, kv_heads) == row // (heads // kv_heads)
    own = jnp.concatenate([own, own], 0)
    diagonal = row == lane

    def scores(i):
        q = q_ref[i].astype(jnp.float32)
        zero = jnp.zeros_like(q)
        both = jnp.concatenate([jnp.concatenate([q, zero], 1), jnp.concatenate([zero, q], 1)], 0).astype(jnp.bfloat16)
        slot = lax.rem(i, SLOTS)
        high = None
        for part in range(2):
            keys = jnp.concatenate(
                [k_buf[slot, pl.ds(part * quarter, quarter)], k_buf[slot, pl.ds(half + part * quarter, quarter)]], 1
            )
            s = lax.dot_general(both, keys, (((1,), (1,)), ((), ())), preferred_element_type=jnp.float32)
            for j in range(quarter // LANES):
                block = jnp.where(own, s[:, j * LANES : (j + 1) * LANES], -jnp.inf)
                s_buf[:, pl.ds(part * quarter + j * LANES, LANES)] = block
                high = block if high is None else jnp.maximum(high, block)
        m_buf[...] = jnp.maximum(high[:heads], high[heads:])

    def weigh():
        m = jnp.broadcast_to(jnp.max(m_buf[...], 1, keepdims=True), (heads, LANES))
        high = jnp.concatenate([m, m], 0)
        total = None
        for j in range(blocks):
            at = pl.ds(j * LANES, LANES)
            w = jnp.exp2((s_buf[:, at] - high) * c)
            total = w if total is None else total + w
            w_buf[:, at] = w.astype(jnp.bfloat16)
        return m, jnp.sum(total[:heads] + total[heads:], 1, keepdims=True)

    def attend(i, m, total):
        slot = lax.rem(i, SLOTS)
        seen = None
        for part in range(2):
            values = jnp.concatenate(
                [v_buf[slot, pl.ds(part * quarter, quarter)], v_buf[slot, pl.ds(half + part * quarter, quarter)]], 1
            )
            r = jnp.dot(w_buf[:, pl.ds(part * quarter, quarter)], values, preferred_element_type=jnp.float32)
            r = r[:heads, :head] + r[heads:, head:]
            seen = r if seen is None else seen + r
        parts[i, me] = seen.astype(jnp.bfloat16)
        m_row = jnp.sum(jnp.where(diagonal, m, 0.0), 0, keepdims=True)
        l_row = jnp.sum(jnp.where(diagonal, total, 0.0), 0, keepdims=True)
        stats[i, me] = jnp.concatenate([m_row, l_row], 1)

    def remote(ref, i, owner, peer, send_sem, recv_sem):
        return pltpu.make_async_remote_copy(
            ref.at[i, owner], ref.at[i, owner], send_sem.at[i], recv_sem.at[i], device_id={"sp": peer}, device_id_type=MESH
        )

    def send(i, peer):
        remote(stats, i, me, peer, ss_sem, sr_sem).start()
        remote(parts, i, me, peer, ps_sem, pr_sem).start()

    def arrived(ref, i, count, sem):
        at = ref.at[i, pl.ds(0, count)]
        pltpu.make_async_copy(at, at, sem.at[i]).wait()

    def sent(i, count):
        arrived(stats, i, count, ss_sem)
        arrived(parts, i, count, ps_sem)

    def peers(do):
        for t in range(1, n):
            do(lax.rem(me + t, n))

    def combine(i):
        arrived(stats, i, n - 1, sr_sem)
        arrived(parts, i, n - 1, pr_sem)
        m = stats[i, :, 0, pl.ds(0, LANES)]
        l = stats[i, :, 0, pl.ds(LANES, LANES)]
        w = jnp.exp2((m - jnp.max(m, 0, keepdims=True)) * c)
        factor = w / jnp.sum(w * l, 0, keepdims=True)
        columns = factor.T
        out = None
        for d in range(n):
            r = parts[i, d].astype(jnp.float32) * columns[:heads, d : d + 1]
            out = r if out is None else out + r
        o_ref[i] = out.astype(o_ref.dtype)

    def share(i, peer):
        return pltpu.make_async_remote_copy(
            o_ref.at[i], o_ref.at[i], os_sem.at[i], or_sem.at[i], device_id={"sp": peer}, device_id_type=MESH
        )

    def shared(i):
        at = o_ref.at[pl.ds(0, n - 1)]
        pltpu.make_async_copy(at, at, os_sem.at[i]).wait()

    def exchange(i):
        @pl.when(jnp.logical_and(i >= 2, jnp.logical_and(i - 2 < split, lax.rem(i - 2, n) != me)))
        def _():
            send(i - 2, lax.rem(i - 2, n))

        @pl.when(i - 2 >= split)
        def _():
            peers(lambda peer: send(i - 2, peer))

        j = i - LAG

        @pl.when(jnp.logical_and(j >= 0, j < split))
        def _():
            @pl.when(lax.rem(j, n) == me)
            def _():
                combine(j)

            @pl.when(lax.rem(j, n) != me)
            def _():
                sent(j, 1)

        @pl.when(jnp.logical_and(j >= 1, j - 1 < split))
        def _():
            @pl.when(lax.rem(j - 1, n) == me)
            def _():
                peers(lambda peer: share(j - 1, peer).start())

    k_copy(0).start()
    k_copy(1).start()
    for i in range(SLOTS - 2):
        for part in range(2):
            v_copy(i, part).start()
        k_copy(i + 2).start()
    for i in range(SLOTS - 2, SLOTS):
        for part in range(2):
            v_copy(i, part).start()

    barrier = pltpu.get_barrier_semaphore()
    for t in range(1, n):
        pl.semaphore_signal(barrier, inc=1, device_id={"sp": lax.rem(me + t, n)}, device_id_type=MESH)

    k_copy(0).wait()
    scores(0)

    @pl.when(SLOTS < batch)
    def _():
        k_copy(SLOTS).start()

    pl.semaphore_wait(barrier, n - 1)

    @pl.loop(1, batch)
    def _(i):
        exchange(i)
        k_copy(i).wait()
        for part in range(2):
            v_copy(i - 1, part).wait()
        m, total = weigh()
        scores(i)
        attend(i - 1, m, total)

        @pl.when(i + SLOTS < batch)
        def _():
            k_copy(i + SLOTS).start()

        @pl.when(i - 1 + SLOTS < batch)
        def _():
            for part in range(2):
                v_copy(i - 1 + SLOTS, part).start()

    peers(lambda peer: send(batch - 2, peer))
    m, total = weigh()
    for part in range(2):
        v_copy(batch - 1, part).wait()
    attend(batch - 1, m, total)
    peers(lambda peer: send(batch - 1, peer))

    @pl.loop(split, batch)
    def _(i):
        combine(i)
        sent(i, n - 1)

    @pl.loop(0, split)
    def _(i):
        @pl.when(lax.rem(i, n) == me)
        def _():
            shared(i)

        @pl.when(lax.rem(i, n) != me)
        def _():
            share(i, me).wait_recv()


def solution(mesh):
    n = mesh.shape["sp"]

    def step(q, k, v):
        batch, heads, head = q.shape
        tokens, kv_heads = k.shape[1:3]
        rows = tokens * kv_heads
        k, v = k.reshape(batch, rows, head), v.reshape(batch, rows, head)
        return pl.pallas_call(
            functools.partial(kernel, n, kv_heads),
            out_shape=jax.ShapeDtypeStruct(q.shape, q.dtype),
            in_specs=[
                pl.BlockSpec(memory_space=pltpu.VMEM),
                pl.BlockSpec(memory_space=pl.ANY),
                pl.BlockSpec(memory_space=pl.ANY),
            ],
            out_specs=pl.BlockSpec(memory_space=pltpu.VMEM),
            scratch_shapes=[
                pltpu.VMEM((SLOTS, rows, head), jnp.bfloat16),
                pltpu.VMEM((SLOTS, rows, head), jnp.bfloat16),
                pltpu.VMEM((2 * heads, rows // 2), jnp.float32),
                pltpu.VMEM((2 * heads, rows // 2), jnp.bfloat16),
                pltpu.VMEM((heads, LANES), jnp.float32),
                pltpu.VMEM((batch, n, heads, head), jnp.bfloat16),
                pltpu.VMEM((batch, n, 1, 2 * LANES), jnp.float32),
                pltpu.SemaphoreType.DMA((SLOTS,)),
                pltpu.SemaphoreType.DMA((SLOTS, 2)),
                pltpu.SemaphoreType.DMA((batch,)),
                pltpu.SemaphoreType.DMA((batch,)),
                pltpu.SemaphoreType.DMA((batch,)),
                pltpu.SemaphoreType.DMA((batch,)),
                pltpu.SemaphoreType.DMA((batch,)),
                pltpu.SemaphoreType.DMA((batch,)),
            ],
            compiler_params=pltpu.CompilerParams(collective_id=0, has_side_effects=True, vmem_limit_bytes=60 * 2**20),
        )(q, k, v)

    return jax.shard_map(
        step,
        mesh=mesh,
        in_specs=(P("dp", None, None), P("dp", "sp", None, None), P("dp", "sp", None, None)),
        out_specs=P("dp", None, None),
        check_vma=False,
    )
```

time: 157 us -> 58.1 us (0.37)
  waiting for transfers between devices: 67 us -> 0 us
  Pallas kernels: 0 us -> 56.3 us
  matrix products: 52.8 us -> 0 us
  between operations: 13.5 us -> 0.01 us
  local copies, waits for them, and re-layouts: 12.6 us -> 1.62 us
  other arithmetic: 10.9 us -> 0 us
    all_gather x1 -> x0, waiting for transfers between devices: 66.9 us -> none  [step(): return together(lax.all_gather(part_of(q, k, v), 'sp')).reshape(q.shape)]
    pallas_call x0 -> x1, Pallas kernels: none -> 56.3 us  [step(): pl.pallas_call(functools.partial(kernel, n, kv_heads), out_shape=jax.Shap...]
    dot_general x2 -> x0, matrix products: 52.8 us -> none  [einsum(): return jnp.einsum(form, a.astype(jnp.float32), b.astype(jnp.float32))]
    slice x1 -> x0, other arithmetic: 5.73 us -> none  [together(): seen, total, high = (parts[..., :-2], parts[..., -2:-1], parts[..., -1:])]
    unnamed x6 -> x1, local copies, waits for them, and re-layouts: 7.13 us -> 1.62 us
    reduce_sum x3 -> x0, other arithmetic: 4.57 us -> none  [the longest x1 2.45 us: together(): jnp.sum(seen * scale, 0) / jnp.sum(total * scale, 0)]
    broadcast_in_dim x2 -> x0, local copies, waits for them, and re-layouts: 3.33 us -> none  [the longest x1 1.66 us: part_of(): jnp.sum(weights, -1, keepdims=True)]
  transfers between devices with their start and end apart: 1 -> 0, of which waited for: 1 -> 0; matrix products, arithmetic and copies ran while one was open for 0% -> 0% of each run, Pallas kernels for 0% -> 0%
where the time goes in v1:
time: 58.1 us; the launch traced here: 57.9 us
  Pallas kernels  56.3 us (97%)
  local copies, waits for them, and re-layouts  1.62 us (3%)
    pallas_call x1, Pallas kernels, step(): pl.pallas_call(functools.partial(kernel, n, kv_heads), out_shape=jax.Shap...  56.3 us
    unnamed x1, local copies, waits for them, and re-layouts  1.62 us

profile of v1, /device:TPU:0, one launch (start us, length us, event | category | flops | bytes accessed | tf_op | source)
XLA Modules:
  0.0 57.9 jit_solution(9946891317988688574)
XLA Ops:
  0.0 56.3 %shard_map.37 = bf16[32,24,128]{2,1,0:T(8,128)(2,1)} custom-call(bf16[32,24,128]{2,1,0:T(8,128)(2,1)} %q_ref.1, bf16[32,8192,128]{2,1,0:T(8,128)(2,1)} %bitcast.k_ref, bf16[32,8192,128]{2,1,0:T(8,128)(2,1)} %bitcast.1.v_ref), custom_call_target="tpu_custom_call" | custom-call | tf_op jit(solution)/shard_map/pallas_call | solution.py:229
  56.3 1.6 %copy.5 = bf16[32,24,128]{2,1,0:T(8,128)(2,1)} copy(bf16[32,24,128]{2,1,0:T(8,128)(2,1)} %shard_map.37) | data formatting | bytes 393216

commit v2 on v0

v2 whole, which is shorter than its diff:
```python
import functools
import math

import jax
import jax.numpy as jnp
from jax import lax
from jax.experimental import pallas as pl
from jax.experimental.pallas import tpu as pltpu
from jax.sharding import PartitionSpec as P

MESH = pl.DeviceIdType.MESH
LANES = 128
SLOTS = 6
TAIL = 4
LAG = 2


def kernel(
    n, kv_heads, q_hbm, k_ref, v_ref, o_ref, q_ref, k_buf, v_buf, s_buf, w_buf, m_buf, parts, stats,
    q_sem, k_sem, v_sem, ps_sem, pr_sem, ss_sem, sr_sem, os_sem, or_sem,
):
    batch, heads, head = q_ref.shape
    rows = k_ref.shape[1]
    half = rows // 2
    quarter = rows // 4
    pairs = batch // 2
    split = pairs - TAIL
    c = head**-0.5 * math.log2(math.e)
    me = lax.axis_index("sp")

    def q_copy():
        return pltpu.make_async_copy(q_hbm, q_ref, q_sem)

    def k_copy(i):
        return pltpu.make_async_copy(k_ref.at[i], k_buf.at[lax.rem(i, SLOTS)], k_sem.at[lax.rem(i, SLOTS)])

    def v_copy(i, part):
        at = pl.ds(part * half, half)
        slot = lax.rem(i, SLOTS)
        return pltpu.make_async_copy(v_ref.at[i, at], v_buf.at[slot, at], v_sem.at[slot, part])

    def v_start(i):
        for part in range(2):
            v_copy(i, part).start()

    def v_wait(i):
        for part in range(2):
            v_copy(i, part).wait()

    row = lax.broadcasted_iota(jnp.int32, (heads, LANES), 0)
    lane = lax.broadcasted_iota(jnp.int32, (heads, LANES), 1)
    own = lax.rem(lane, kv_heads) == row // (heads // kv_heads)
    own = jnp.concatenate([own, own], 0)
    diagonal = row == lane

    def side_by_side(buf, slot, part):
        return jnp.concatenate([buf[slot, pl.ds(part * half, quarter)], buf[slot, pl.ds(part * half + quarter, quarter)]], 1)

    def scores(i):
        q = q_ref[i].astype(jnp.float32)
        zero = jnp.zeros_like(q)
        both = jnp.concatenate([jnp.concatenate([q, zero], 1), jnp.concatenate([zero, q], 1)], 0).astype(jnp.bfloat16)
        high = None
        for part in range(2):
            keys = side_by_side(k_buf, lax.rem(i, SLOTS), part)
            s = lax.dot_general(both, keys, (((1,), (1,)), ((), ())), preferred_element_type=jnp.float32)
            for j in range(quarter // LANES):
                block = jnp.where(own, s[:, j * LANES : (j + 1) * LANES], -jnp.inf)
                s_buf[:, pl.ds(part * quarter + j * LANES, LANES)] = block
                high = block if high is None else jnp.maximum(high, block)
        m_buf[...] = jnp.maximum(high[:heads], high[heads:])

    def weigh(turn):
        m = jnp.broadcast_to(jnp.max(m_buf[...], 1, keepdims=True), (heads, LANES))
        high = jnp.concatenate([m, m], 0)
        total = None
        for j in range(half // LANES):
            at = pl.ds(j * LANES, LANES)
            w = jnp.exp2((s_buf[:, at] - high) * c)
            total = w if total is None else total + w
            w_buf[turn, :, at] = w.astype(jnp.bfloat16)
        return m, jnp.sum(total[:heads] + total[heads:], 1, keepdims=True)

    def keep(i, m, total):
        m_row = jnp.sum(jnp.where(diagonal, m, 0.0), 0, keepdims=True)
        l_row = jnp.sum(jnp.where(diagonal, total, 0.0), 0, keepdims=True)
        stats[i, me] = jnp.concatenate([m_row, l_row], 1)

    def attend(i, turn, part):
        values = side_by_side(v_buf, lax.rem(i, SLOTS), part)
        r = jnp.dot(w_buf[turn, :, pl.ds(part * quarter, quarter)], values, preferred_element_type=jnp.float32)
        return r[:heads, :head] + r[heads:, head:]

    def attend_all(i, turn):
        parts[i, me] = (attend(i, turn, 0) + attend(i, turn, 1)).astype(jnp.bfloat16)

    def remote(ref, first, count, p, peer, send_sem, recv_sem):
        at = ref.at[pl.ds(first, count), me]
        return pltpu.make_async_remote_copy(at, at, send_sem.at[p], recv_sem.at[p], device_id={"sp": peer}, device_id_type=MESH)

    def send(first, count, p, peer):
        remote(stats, first, count, p, peer, ss_sem, sr_sem).start()
        remote(parts, first, count, p, peer, ps_sem, pr_sem).start()

    def peers(do):
        upper = me >= n // 2
        mine = jnp.where(upper, me, n - 1 - me)
        for t in range(n - 1):
            d = jnp.where(t >= mine, t + 1, t)
            do(jnp.where(upper, d, n - 1 - d))

    def finish(ref, first, count, times, sem):
        at = ref.at[pl.ds(first, count), pl.ds(0, times)]
        pltpu.make_async_copy(at, at, sem).wait()

    def sent(first, count, p, times):
        finish(stats, first, count, times, ss_sem.at[p])
        finish(parts, first, count, times, ps_sem.at[p])

    def combine(first, count, p):
        finish(stats, first, count, n - 1, sr_sem.at[p])
        finish(parts, first, count, n - 1, pr_sem.at[p])
        for i in range(count):
            i = first + i
            m = stats[i, :, 0, pl.ds(0, LANES)]
            l = stats[i, :, 0, pl.ds(LANES, LANES)]
            w = jnp.exp2((m - jnp.max(m, 0, keepdims=True)) * c)
            columns = (w / jnp.sum(w * l, 0, keepdims=True)).T
            out = None
            for d in range(n):
                r = parts[i, d].astype(jnp.float32) * columns[:heads, d : d + 1]
                out = r if out is None else out + r
            o_ref[i] = out.astype(o_ref.dtype)

    def share(p, peer):
        at = o_ref.at[pl.ds(2 * p, 2)]
        return pltpu.make_async_remote_copy(at, at, os_sem.at[p], or_sem.at[p], device_id={"sp": peer}, device_id_type=MESH)

    def share_all(p):
        @pl.when(jnp.logical_and(jnp.logical_and(p >= 0, p < split), lax.rem(p, n) == me))
        def _():
            peers(lambda peer: share(p, peer).start())

    def exchange(p):
        owner = lax.rem(jnp.maximum(p, 0), n)

        @pl.when(jnp.logical_and(jnp.logical_and(p >= 0, p < split), owner != me))
        def _():
            send(2 * p, 2, p, owner)

        @pl.when(p >= split)
        def _():
            peers(lambda peer: send(2 * p, 2, p, peer))

        share_all(p - LAG - 1)
        ready = p - LAG

        @pl.when(jnp.logical_and(jnp.logical_and(ready >= 0, ready < split), lax.rem(jnp.maximum(ready, 0), n) == me))
        def _():
            combine(2 * ready, 2, ready)

    k_copy(0).start()
    q_copy().start()
    k_copy(1).start()
    v_start(0)
    k_copy(2).start()
    v_start(1)

    barrier = pltpu.get_barrier_semaphore()
    for t in range(1, n):
        pl.semaphore_signal(barrier, inc=1, device_id={"sp": lax.rem(me + t, n)}, device_id_type=MESH)

    q_copy().wait()
    k_copy(0).wait()
    for i in range(2, SLOTS - 2):
        k_copy(i + 1).start()
        v_start(i)
    scores(0)
    for i in range(SLOTS - 2, SLOTS):
        k_copy(i + 1).start()
        v_start(i)
    pl.semaphore_wait(barrier, n - 1)

    @pl.loop(0, pairs - 1)
    def _(p):
        i = 2 * p + 1
        exchange(p - 1)
        for t in range(2):
            k_copy(i + t).wait()
            v_wait(i - 1 + t)
        for t in range(2):
            m, total = weigh(t)
            scores(i + t)
            attend_all(i - 1 + t, t)
            keep(i - 1 + t, m, total)

        for t in range(2):

            @pl.when(i + t + SLOTS < batch)
            def _():
                k_copy(i + t + SLOTS).start()

            @pl.when(i - 1 + t + SLOTS < batch)
            def _():
                v_start(i - 1 + t + SLOTS)

    last = batch - 1
    exchange(jnp.int32(pairs - 2))
    k_copy(last).wait()
    m, total = weigh(0)
    scores(last)
    keep(last - 1, m, total)
    v_wait(last - 1)
    m, total = weigh(1)
    attend_all(last - 1, 0)
    keep(last, m, total)
    peers(lambda peer: send(last - 1, 1, pairs - 1, peer))
    v_copy(last, 0).wait()
    r = attend(last, 1, 0)
    v_copy(last, 1).wait()
    parts[last, me] = (r + attend(last, 1, 1)).astype(jnp.bfloat16)
    peers(lambda peer: send(last, 1, pairs, peer))

    @pl.loop(split, pairs - 1)
    def _(p):
        combine(2 * p, 2, p)
        sent(2 * p, 2, p, n - 1)

    @pl.loop(0, split)
    def _(p):
        @pl.when(lax.rem(p, n) == me)
        def _():
            at = o_ref.at[pl.ds(0, 2 * (n - 1))]
            pltpu.make_async_copy(at, at, os_sem.at[p]).wait()

        @pl.when(lax.rem(p, n) != me)
        def _():
            sent(2 * p, 2, p, 1)
            share(p, me).wait_recv()

    combine(last - 1, 1, pairs - 1)
    sent(last - 1, 1, pairs - 1, n - 1)
    sent(last, 1, pairs, n - 1)
    combine(last, 1, pairs)


def solution(mesh):
    n = mesh.shape["sp"]

    def step(q, k, v):
        batch, heads, head = q.shape
        tokens, kv_heads = k.shape[1:3]
        rows = tokens * kv_heads
        k, v = k.reshape(batch, rows, head), v.reshape(batch, rows, head)
        return pl.pallas_call(
            functools.partial(kernel, n, kv_heads),
            out_shape=pltpu.VMEM(q.shape, q.dtype),
            in_specs=[pl.BlockSpec(memory_space=pl.ANY)] * 3,
            out_specs=pl.BlockSpec(memory_space=pltpu.VMEM),
            scratch_shapes=[
                pltpu.VMEM((batch, heads, head), jnp.bfloat16),
                pltpu.VMEM((SLOTS, rows, head), jnp.bfloat16),
                pltpu.VMEM((SLOTS, rows, head), jnp.bfloat16),
                pltpu.VMEM((2 * heads, rows // 2), jnp.float32),
                pltpu.VMEM((2, 2 * heads, rows // 2), jnp.bfloat16),
                pltpu.VMEM((heads, LANES), jnp.float32),
                pltpu.VMEM((batch, n, heads, head), jnp.bfloat16),
                pltpu.VMEM((batch, n, 1, 2 * LANES), jnp.float32),
                pltpu.SemaphoreType.DMA,
                pltpu.SemaphoreType.DMA((SLOTS,)),
                pltpu.SemaphoreType.DMA((SLOTS, 2)),
            ]
            + [pltpu.SemaphoreType.DMA((batch // 2 + 1,))] * 6,
            compiler_params=pltpu.CompilerParams(collective_id=0, has_side_effects=True, vmem_limit_bytes=56 * 2**20),
        )(q, k, v)

    return jax.shard_map(
        step,
        mesh=mesh,
        in_specs=(P("dp", None, None), P("dp", "sp", None, None), P("dp", "sp", None, None)),
        out_specs=P("dp", None, None),
        check_vma=False,
    )
```

time: 157 us -> 52.5 us (0.33)
  waiting for transfers between devices: 67 us -> 0 us
  matrix products: 52.8 us -> 0 us
  Pallas kernels: 0 us -> 51.7 us
  between operations: 13.5 us -> 0.01 us
  local copies, waits for them, and re-layouts: 12.6 us -> 0.68 us
  other arithmetic: 10.9 us -> 0 us
    all_gather x1 -> x0, waiting for transfers between devices: 66.9 us -> none  [step(): return together(lax.all_gather(part_of(q, k, v), 'sp')).reshape(q.shape)]
    dot_general x2 -> x0, matrix products: 52.8 us -> none  [einsum(): return jnp.einsum(form, a.astype(jnp.float32), b.astype(jnp.float32))]
    pallas_call x0 -> x1, Pallas kernels: none -> 51.7 us  [step(): pl.pallas_call(functools.partial(kernel, n, kv_heads), out_shape=pltpu.VM...]
    unnamed x6 -> x1, local copies, waits for them, and re-layouts: 7.13 us -> 0.68 us
    slice x1 -> x0, other arithmetic: 5.73 us -> none  [together(): seen, total, high = (parts[..., :-2], parts[..., -2:-1], parts[..., -1:])]
    reduce_sum x3 -> x0, other arithmetic: 4.57 us -> none  [the longest x1 2.45 us: together(): jnp.sum(seen * scale, 0) / jnp.sum(total * scale, 0)]
    broadcast_in_dim x2 -> x0, local copies, waits for them, and re-layouts: 3.33 us -> none  [the longest x1 1.66 us: part_of(): jnp.sum(weights, -1, keepdims=True)]
  transfers between devices with their start and end apart: 1 -> 0, of which waited for: 1 -> 0; matrix products, arithmetic and copies ran while one was open for 0% -> 0% of each run, Pallas kernels for 0% -> 0%
where the time goes in v2:
time: 52.5 us; the launch traced here: 52.4 us
  Pallas kernels  51.7 us (98%)
  local copies, waits for them, and re-layouts  0.68 us (1%)
    pallas_call x1, Pallas kernels, step(): pl.pallas_call(functools.partial(kernel, n, kv_heads), out_shape=pltpu.VM...  51.7 us

profile of v2, /device:TPU:0, one launch (start us, length us, event | category | flops | bytes accessed | tf_op | source)
XLA Modules:
  0.0 52.4 jit_solution(5975400213913278034)
XLA Ops:
  0.0 51.7 %shard_map.37 = bf16[32,24,128]{2,1,0:T(8,128)(2,1)S(1)} custom-call(bf16[32,24,128]{2,1,0:T(8,128)(2,1)} %q_hbm.1, bf16[32,8192,128]{2,1,0:T(8,128)(2,1)} %bitcast.k_ref, bf16[32,8192,128]{2,1,0:T(8,128)(2,1)} %bitcast.1.v_ref), custom_call_target="tpu_custom_call" | custom-call | tf_op jit(solution)/shard_map/pallas_call | solution.py:255
  51.7 0.7 %copy.5 = bf16[32,24,128]{2,1,0:T(8,128)(2,1)} copy(bf16[32,24,128]{2,1,0:T(8,128)(2,1)S(1)} %shard_map.37) | data formatting | bytes 393216
